TPU v7x, 8 devices: a whole 2x2x1 slice. The times are simulated.
8 devices in a mesh: batch: 1 (over z), cy: 2 (over y), cx: 4 (over x, core).
Axes of the slice: x: 2, y: 2, z: 1, core: 2. Of those that a mesh axis runs over, the one named last changes fastest.
Arguments:
- q_seq: bfloat16 [8192, 16, 256], P(('batch', 'cx', 'cy'))
- k_seq: bfloat16 [8192, 16, 256], P(('batch', 'cx', 'cy'))
- v_seq: bfloat16 [8192, 16, 256], P(('batch', 'cx', 'cy'))
Outputs:
- output: bfloat16 [8192, 16, 256], P(('batch', 'cx', 'cy'))
All inputs are finite; a program needn't handle non-finite values.
Results may differ from a plain program's by a relative error of at most 0.004836.
Values are sent between devices in bfloat16 or wider.
A program may use at most 1 GiB of HBM per device.

v0:
```python
import math
import jax
import jax.numpy as jnp
from jax import lax
from jax.sharding import PartitionSpec as P


def block_update(running, q_grouped, k_blk, v_blk):
    row_max, row_sum, out_acc = running
    score_scale = 1.0 / math.sqrt(q_grouped.shape[-1])
    scores = jnp.einsum("qkgd,skd->kgqs", q_grouped, k_blk, preferred_element_type=jnp.float32) * score_scale
    new_max = jnp.maximum(row_max, jnp.max(scores, axis=-1))
    rescale = jnp.exp(row_max - new_max)
    prob_blk = jnp.exp(scores - new_max[..., None])
    row_sum = row_sum * rescale + jnp.sum(prob_blk, axis=-1)
    weighted = jnp.einsum("kgqs,skd->kgqd", prob_blk.astype(jnp.bfloat16), v_blk, preferred_element_type=jnp.float32)
    out_acc = out_acc * rescale[..., None] + weighted
    return new_max, row_sum, out_acc


def start_state(q_grouped):
    tokens, num_kv, groups, head_dim = q_grouped.shape
    row_max = jnp.full((num_kv, groups, tokens), -jnp.inf, jnp.float32)
    row_sum = jnp.zeros((num_kv, groups, tokens), jnp.float32)
    out_acc = jnp.zeros((num_kv, groups, tokens, head_dim), jnp.float32)
    return row_max, row_sum, out_acc


def finish(running, tokens, num_heads, head_dim):
    row_max, row_sum, out_acc = running
    result = out_acc / row_sum[..., None]
    return jnp.transpose(result, (2, 0, 1, 3)).reshape(tokens, num_heads, head_dim).astype(jnp.bfloat16)


def solution(mesh):
    size_x = mesh.shape["cx"]
    size_y = mesh.shape["cy"]
    seq_spec = P(("batch", "cx", "cy"), None, None)
    perm_x = [(dev_idx, (dev_idx + 1) % size_x) for dev_idx in range(size_x)]
    perm_y = [(dev_idx, (dev_idx + 1) % size_y) for dev_idx in range(size_y)]

    def local_attention(q_local, k_local, v_local):
        tokens, num_heads, head_dim = q_local.shape
        num_kv = k_local.shape[1]
        q_grouped = q_local.reshape(tokens, num_kv, num_heads // num_kv, head_dim)

        def step_x(step_idx, loop_state):
            running, k_blk, v_blk = loop_state
            running = block_update(running, q_grouped, k_blk, v_blk)
            k_blk = lax.ppermute(k_blk, "cx", perm_x)
            v_blk = lax.ppermute(v_blk, "cx", perm_x)
            return running, k_blk, v_blk

        def sweep_x(loop_state):
            running, k_blk, v_blk = lax.fori_loop(0, size_x - 1, step_x, loop_state)
            return block_update(running, q_grouped, k_blk, v_blk), k_blk, v_blk

        def step_y(step_idx, loop_state):
            running, k_blk, v_blk = sweep_x(loop_state)
            k_blk = lax.ppermute(k_blk, "cy", perm_y)
            v_blk = lax.ppermute(v_blk, "cy", perm_y)
            return running, k_blk, v_blk

        loop_state = lax.fori_loop(0, size_y - 1, step_y, (start_state(q_grouped), k_local, v_local))
        running = sweep_x(loop_state)[0]
        return finish(running, tokens, num_heads, head_dim)

    return jax.shard_map(local_attention, mesh=mesh, in_specs=(seq_spec, seq_spec, seq_spec), out_specs=seq_spec, check_vma=False)
```

profile of v0, /device:TPU:0, one launch (start us, length us, event | category | flops | bytes accessed | tf_op | source)
XLA Modules:
  0.0 1632.4 jit_solution(3511710076828986120)
XLA Ops:
  29.1 571.4 %while.53 = (s32[]{:T(128)}, f32[16,1,1024]{2,0,1:T(8,128)S(1)}, f32[16,1,1024]{2,0,1:T(8,128)S(1)}, f32[16,1,1024,256]{3,2,0,1:T(8,128)}, bf16[1024,16,256]{2,0...) while((s32[]{:T(128)}, f32[16,1,1024]{2,0,1:T(8,128)S(1)}, ...), condition=%wide.region_3.4_spmd.clone, body=%wide.region_0.3_spmd.clone.sunk | while | flops 17326768128 | bytes 361758848 | solution.py:55
  47.4 28.6 %bitcast_reduce_fusion.7 = (f32[16,1024]{1,0:T(8,128)S(1)}, f32[16,1024,1024]{2,1,0:T(8,128)}) fusion(bf16[1024,16,256]{2,0,1:T(8,128)(2,1)} %copy.38, bf16[1024,16,1,256]{3,0,1,2:T(8,128)(2,1)} %get-tuple-element.319), kind=kOutput, calls=%fused_computation.18.clone.1 | convolution fusion | flops 8623472640 | bytes 83951616 | tf_op jit(solution)/shard_map/while/body/eval_jaxpr/while/body/eval_jaxpr/qkgd,skd->kgqs/dot_general | solution.py:11
  97.4 34.1 %bitcast_add_fusion.15 = f32[16,1,1024,256]{3,2,0,1:T(8,128)} fusion(f32[16,1,1024,256]{3,2,0,1:T(8,128)} %get-tuple-element.307, bf16[1024,16,256]{2,0,1:T(8,128)(2,1)} %copy.39, f32[16,1024,1024]{2,1,0:T(8,128)} %get-tuple-element.293, f32[16,1024]{1,0:T(8,128)S(1)} %bitcast.224, f32[16,1024]{1,0:T(8,128)S(1)} %get-tuple-element.294, pred[]{:T(512)S(6)} %compare.3), kind=kOutput, calls=%fused_computation.26.clone.1 | convolution fusion | flops 8652849152 | bytes 109182976 | tf_op jit(solution)/shard_map/while/body/eval_jaxpr/while/body/eval_jaxpr/kgqs,skd->kgqd/dot_general | solution.py:16
  131.5 88.8 %collective-permute-done.3 = bf16[1024,16,256]{2,0,1:T(8,128)(2,1)} collective-permute-done((bf16[1024,16,256]{2,0,1:T(8,128)(2,1)}, bf16[1024,16,256]{2,0,1:T(8,128)(2,1)}, u32[]{:S(2)}, u32[]{:S(2)}) %collective-permute-start.3) | collective-permute-done | bytes 8388640 | tf_op jit(solution)/shard_map/while/body/eval_jaxpr/while/body/eval_jaxpr/ppermute | solution.py:51
  237.4 28.6 %bitcast_reduce_fusion.7 = (f32[16,1024]{1,0:T(8,128)S(1)}, f32[16,1024,1024]{2,1,0:T(8,128)}) fusion(bf16[1024,16,256]{2,0,1:T(8,128)(2,1)} %copy.38, bf16[1024,16,1,256]{3,0,1,2:T(8,128)(2,1)} %get-tuple-element.319), kind=kOutput, calls=%fused_computation.18.clone.1 | convolution fusion | flops 8623472640 | bytes 83951616 | tf_op jit(solution)/shard_map/while/body/eval_jaxpr/while/body/eval_jaxpr/qkgd,skd->kgqs/dot_general | solution.py:11
  287.5 37.4 %bitcast_add_fusion.15 = f32[16,1,1024,256]{3,2,0,1:T(8,128)} fusion(f32[16,1,1024,256]{3,2,0,1:T(8,128)} %get-tuple-element.307, bf16[1024,16,256]{2,0,1:T(8,128)(2,1)} %copy.39, f32[16,1024,1024]{2,1,0:T(8,128)} %get-tuple-element.293, f32[16,1024]{1,0:T(8,128)S(1)} %bitcast.224, f32[16,1024]{1,0:T(8,128)S(1)} %get-tuple-element.294, pred[]{:T(512)S(6)} %compare.3), kind=kOutput, calls=%fused_computation.26.clone.1 | convolution fusion | flops 8652849152 | bytes 109182976 | tf_op jit(solution)/shard_map/while/body/eval_jaxpr/while/body/eval_jaxpr/kgqs,skd->kgqd/dot_general | solution.py:16
  324.9 85.5 %collective-permute-done.3 = bf16[1024,16,256]{2,0,1:T(8,128)(2,1)} collective-permute-done((bf16[1024,16,256]{2,0,1:T(8,128)(2,1)}, bf16[1024,16,256]{2,0,1:T(8,128)(2,1)}, u32[]{:S(2)}, u32[]{:S(2)}) %collective-permute-start.3) | collective-permute-done | bytes 8388640 | tf_op jit(solution)/shard_map/while/body/eval_jaxpr/while/body/eval_jaxpr/ppermute | solution.py:51
  427.5 28.6 %bitcast_reduce_fusion.7 = (f32[16,1024]{1,0:T(8,128)S(1)}, f32[16,1024,1024]{2,1,0:T(8,128)}) fusion(bf16[1024,16,256]{2,0,1:T(8,128)(2,1)} %copy.38, bf16[1024,16,1,256]{3,0,1,2:T(8,128)(2,1)} %get-tuple-element.319), kind=kOutput, calls=%fused_computation.18.clone.1 | convolution fusion | flops 8623472640 | bytes 83951616 | tf_op jit(solution)/shard_map/while/body/eval_jaxpr/while/body/eval_jaxpr/qkgd,skd->kgqs/dot_general | solution.py:11
  477.6 37.4 %bitcast_add_fusion.15 = f32[16,1,1024,256]{3,2,0,1:T(8,128)} fusion(f32[16,1,1024,256]{3,2,0,1:T(8,128)} %get-tuple-element.307, bf16[1024,16,256]{2,0,1:T(8,128)(2,1)} %copy.39, f32[16,1024,1024]{2,1,0:T(8,128)} %get-tuple-element.293, f32[16,1024]{1,0:T(8,128)S(1)} %bitcast.224, f32[16,1024]{1,0:T(8,128)S(1)} %get-tuple-element.294, pred[]{:T(512)S(6)} %compare.3), kind=kOutput, calls=%fused_computation.26.clone.1 | convolution fusion | flops 8652849152 | bytes 109182976 | tf_op jit(solution)/shard_map/while/body/eval_jaxpr/while/body/eval_jaxpr/kgqs,skd->kgqd/dot_general | solution.py:16
  514.9 85.5 %collective-permute-done.3 = bf16[1024,16,256]{2,0,1:T(8,128)(2,1)} collective-permute-done((bf16[1024,16,256]{2,0,1:T(8,128)(2,1)}, bf16[1024,16,256]{2,0,1:T(8,128)(2,1)}, u32[]{:S(2)}, u32[]{:S(2)}) %collective-permute-start.3) | collective-permute-done | bytes 8388640 | tf_op jit(solution)/shard_map/while/body/eval_jaxpr/while/body/eval_jaxpr/ppermute | solution.py:51
  602.8 28.7 %bitcast_reduce_fusion.3 = (f32[16,1024]{1,0:T(8,128)S(1)}, f32[16,1024,1024]{2,1,0:T(8,128)}) fusion(bf16[1024,16,256]{2,0,1:T(8,128)(2,1)} %get-tuple-element.109, bf16[1024,16,256]{2,1,0:T(8,128)(2,1)} %param.7), kind=kOutput, calls=%fused_computation.40 | convolution fusion | flops 8623472640 | bytes 83951616 | tf_op jit(solution)/shard_map/while/body/eval_jaxpr/qkgd,skd->kgqs/dot_general | solution.py:11
  654.4 37.7 %bitcast_add_fusion.5 = f32[16,1,1024,256]{3,2,0,1:T(8,128)} fusion(f32[16,1,1024,256]{3,2,0,1:T(8,128)} %get-tuple-element.111, bf16[1024,16,256]{2,0,1:T(8,128)(2,1)} %get-tuple-element.112, f32[16,1024,1024]{2,1,0:T(8,128)} %get-tuple-element.190, f32[16,1024]{1,0:T(8,128)} %bitcast.15, f32[16,1024]{1,0:T(8,128)S(1)} %get-tuple-element.181), kind=kOutput, calls=%fused_computation.57 | convolution fusion | flops 8648654848 | bytes 109182976 | tf_op jit(solution)/shard_map/while/body/eval_jaxpr/kgqs,skd->kgqd/dot_general | solution.py:16
  692.1 92.0 %collective-permute-done.4 = bf16[1024,16,256]{2,0,1:T(8,128)(2,1)} collective-permute-done((bf16[1024,16,256]{2,0,1:T(8,128)(2,1)}, bf16[1024,16,256]{2,0,1:T(8,128)(2,1)}, u32[]{:S(2)}, u32[]{:S(2)}) %collective-permute-start.4) | collective-permute-done | bytes 8388640 | tf_op jit(solution)/shard_map/while/body/eval_jaxpr/ppermute | solution.py:60
  784.1 178.4 %collective-permute-done.5 = bf16[1024,16,256]{2,0,1:T(8,128)(2,1)} collective-permute-done((bf16[1024,16,256]{2,0,1:T(8,128)(2,1)}, bf16[1024,16,256]{2,0,1:T(8,128)(2,1)}, u32[]{:S(2)}, u32[]{:S(2)}) %collective-permute-start.5) | collective-permute-done | bytes 8388640 | tf_op jit(solution)/shard_map/while/body/eval_jaxpr/ppermute | solution.py:61
  962.5 570.2 %while.52 = (s32[]{:T(128)}, f32[16,1,1024]{2,0,1:T(8,128)}, f32[16,1,1024]{2,0,1:T(8,128)S(1)}, f32[16,1,1024,256]{3,2,0,1:T(8,128)}, bf16[1024,16,256]{2,0,1:T...) while((s32[]{:T(128)}, f32[16,1,1024]{2,0,1:T(8,128)}, ...), condition=%wide.region_9.10_spmd, body=%wide.region_6.9_spmd.sunk | while | flops 17322524672 | bytes 361758848 | solution.py:55
  1030.0 37.3 %bitcast_add_fusion.13 = f32[16,1,1024,256]{3,2,0,1:T(8,128)} fusion(f32[16,1,1024,256]{3,2,0,1:T(8,128)} %get-tuple-element.333, bf16[1024,16,256]{2,0,1:T(8,128)(2,1)} %copy.57, f32[16,1024,1024]{2,1,0:T(8,128)} %get-tuple-element.282, f32[16,1024]{1,0:T(8,128)S(1)} %bitcast.226, f32[16,1024]{1,0:T(8,128)S(1)} %get-tuple-element.283), kind=kOutput, calls=%fused_computation.9.clone.1 | convolution fusion | flops 8648654848 | bytes 109182976 | tf_op jit(solution)/shard_map/while/body/eval_jaxpr/kgqs,skd->kgqd/dot_general | solution.py:16
  1067.3 85.3 %collective-permute-done.1 = bf16[1024,16,256]{2,0,1:T(8,128)(2,1)} collective-permute-done((bf16[1024,16,256]{2,0,1:T(8,128)(2,1)}, bf16[1024,16,256]{2,0,1:T(8,128)(2,1)}, u32[]{:S(2)}, u32[]{:S(2)}) %collective-permute-start.1) | collective-permute-done | bytes 8388640 | tf_op jit(solution)/shard_map/while/body/eval_jaxpr/ppermute | solution.py:51
  1167.7 28.6 %bitcast_reduce_fusion.6 = (f32[16,1024]{1,0:T(8,128)S(1)}, f32[16,1024,1024]{2,1,0:T(8,128)}) fusion(bf16[1024,16,256]{2,0,1:T(8,128)(2,1)} %copy.56, bf16[1024,16,1,256]{3,0,1,2:T(8,128)(2,1)} %get-tuple-element.344), kind=kOutput, calls=%fused_computation.1.clone.1 | convolution fusion | flops 8623472640 | bytes 83951616 | tf_op jit(solution)/shard_map/while/body/eval_jaxpr/qkgd,skd->kgqs/dot_general | solution.py:11
  1220.0 37.3 %bitcast_add_fusion.13 = f32[16,1,1024,256]{3,2,0,1:T(8,128)} fusion(f32[16,1,1024,256]{3,2,0,1:T(8,128)} %get-tuple-element.333, bf16[1024,16,256]{2,0,1:T(8,128)(2,1)} %copy.57, f32[16,1024,1024]{2,1,0:T(8,128)} %get-tuple-element.282, f32[16,1024]{1,0:T(8,128)S(1)} %bitcast.226, f32[16,1024]{1,0:T(8,128)S(1)} %get-tuple-element.283), kind=kOutput, calls=%fused_computation.9.clone.1 | convolution fusion | flops 8648654848 | bytes 109182976 | tf_op jit(solution)/shard_map/while/body/eval_jaxpr/kgqs,skd->kgqd/dot_general | solution.py:16
  1257.4 85.3 %collective-permute-done.1 = bf16[1024,16,256]{2,0,1:T(8,128)(2,1)} collective-permute-done((bf16[1024,16,256]{2,0,1:T(8,128)(2,1)}, bf16[1024,16,256]{2,0,1:T(8,128)(2,1)}, u32[]{:S(2)}, u32[]{:S(2)}) %collective-permute-start.1) | collective-permute-done | bytes 8388640 | tf_op jit(solution)/shard_map/while/body/eval_jaxpr/ppermute | solution.py:51
  1410.1 37.3 %bitcast_add_fusion.13 = f32[16,1,1024,256]{3,2,0,1:T(8,128)} fusion(f32[16,1,1024,256]{3,2,0,1:T(8,128)} %get-tuple-element.333, bf16[1024,16,256]{2,0,1:T(8,128)(2,1)} %copy.57, f32[16,1024,1024]{2,1,0:T(8,128)} %get-tuple-element.282, f32[16,1024]{1,0:T(8,128)S(1)} %bitcast.226, f32[16,1024]{1,0:T(8,128)S(1)} %get-tuple-element.283), kind=kOutput, calls=%fused_computation.9.clone.1 | convolution fusion | flops 8648654848 | bytes 109182976 | tf_op jit(solution)/shard_map/while/body/eval_jaxpr/kgqs,skd->kgqd/dot_general | solution.py:16
  1447.4 85.3 %collective-permute-done.1 = bf16[1024,16,256]{2,0,1:T(8,128)(2,1)} collective-permute-done((bf16[1024,16,256]{2,0,1:T(8,128)(2,1)}, bf16[1024,16,256]{2,0,1:T(8,128)(2,1)}, u32[]{:S(2)}, u32[]{:S(2)}) %collective-permute-start.1) | collective-permute-done | bytes 8388640 | tf_op jit(solution)/shard_map/while/body/eval_jaxpr/ppermute | solution.py:51
  1532.7 28.7 %bitcast_reduce_fusion.2 = (f32[16,1024]{1,0:T(8,128)S(1)}, f32[16,1024,1024]{2,1,0:T(8,128)}) fusion(bf16[1024,16,256]{2,0,1:T(8,128)(2,1)} %get-tuple-element.115, bf16[1024,16,256]{2,1,0:T(8,128)(2,1)} %param.7), kind=kOutput, calls=%fused_computation.37 | convolution fusion | flops 8623472640 | bytes 83951616 | tf_op jit(solution)/shard_map/qkgd,skd->kgqs/dot_general | solution.py:11
  1584.7 35.7 %fusion.54 = bf16[1024,16,256]{2,0,1:T(8,128)(2,1)} fusion(f32[16,1024]{1,0:T(8,128)S(1)} %get-tuple-element.188, bf16[1024,16,256]{2,0,1:T(8,128)(2,1)} %get-tuple-element.116, f32[16,1024,1024]{2,1,0:T(8,128)} %get-tuple-element.192, f32[16,1024]{1,0:T(8,128)S(1)} %fusion.58, f32[16,1,1024,256]{3,2,0,1:T(8,128)} %get-tuple-element.113, ...), kind=kOutput, calls=%fused_computation.63 | convolution fusion | flops 8657043456 | bytes 100859904 | tf_op jit(solution)/shard_map/kgqs,skd->kgqd/dot_general | solution.py:16
  (71 shorter events, 379.8 us)
Async XLA Ops:
  36.5 95.0 %collective-permute-start.2 = (bf16[1024,16,256]{2,0,1:T(8,128)(2,1)}, bf16[1024,16,256]{2,0,1:T(8,128)(2,1)}, u32[]{:S(2)}, u32[]{:S(2)}) collective-permute-start(bf16[1024,16,256]{2,0,1:T(8,128)(2,1)} %copy.38), channel_id=1, source_target_pairs={{0,1},{1,2},{2,3},{3,0},{4,5},{5,6},{6,7},{7,4}} | collective-permute-start | bytes 25165832 | tf_op jit(solution)/shard_map/while/body/eval_jaxpr/while/body/eval_jaxpr/ppermute | solution.py:50
  44.8 175.5 %collective-permute-start.3 = (bf16[1024,16,256]{2,0,1:T(8,128)(2,1)}, bf16[1024,16,256]{2,0,1:T(8,128)(2,1)}, u32[]{:S(2)}, u32[]{:S(2)}) collective-permute-start(bf16[1024,16,256]{2,0,1:T(8,128)(2,1)} %copy.39), channel_id=1, source_target_pairs={{0,1},{1,2},{2,3},{3,0},{4,5},{5,6},{6,7},{7,4}} | collective-permute-start | bytes 25165832 | tf_op jit(solution)/shard_map/while/body/eval_jaxpr/while/body/eval_jaxpr/ppermute | solution.py:51
  227.6 97.3 %collective-permute-start.2 = (bf16[1024,16,256]{2,0,1:T(8,128)(2,1)}, bf16[1024,16,256]{2,0,1:T(8,128)(2,1)}, u32[]{:S(2)}, u32[]{:S(2)}) collective-permute-start(bf16[1024,16,256]{2,0,1:T(8,128)(2,1)} %copy.38), channel_id=1, source_target_pairs={{0,1},{1,2},{2,3},{3,0},{4,5},{5,6},{6,7},{7,4}} | collective-permute-start | bytes 25165832 | tf_op jit(solution)/shard_map/while/body/eval_jaxpr/while/body/eval_jaxpr/ppermute | solution.py:50
  235.0 175.3 %collective-permute-start.3 = (bf16[1024,16,256]{2,0,1:T(8,128)(2,1)}, bf16[1024,16,256]{2,0,1:T(8,128)(2,1)}, u32[]{:S(2)}, u32[]{:S(2)}) collective-permute-start(bf16[1024,16,256]{2,0,1:T(8,128)(2,1)} %copy.39), channel_id=1, source_target_pairs={{0,1},{1,2},{2,3},{3,0},{4,5},{5,6},{6,7},{7,4}} | collective-permute-start | bytes 25165832 | tf_op jit(solution)/shard_map/while/body/eval_jaxpr/while/body/eval_jaxpr/ppermute | solution.py:51
  417.7 97.2 %collective-permute-start.2 = (bf16[1024,16,256]{2,0,1:T(8,128)(2,1)}, bf16[1024,16,256]{2,0,1:T(8,128)(2,1)}, u32[]{:S(2)}, u32[]{:S(2)}) collective-permute-start(bf16[1024,16,256]{2,0,1:T(8,128)(2,1)} %copy.38), channel_id=1, source_target_pairs={{0,1},{1,2},{2,3},{3,0},{4,5},{5,6},{6,7},{7,4}} | collective-permute-start | bytes 25165832 | tf_op jit(solution)/shard_map/while/body/eval_jaxpr/while/body/eval_jaxpr/ppermute | solution.py:50
  425.1 175.3 %collective-permute-start.3 = (bf16[1024,16,256]{2,0,1:T(8,128)(2,1)}, bf16[1024,16,256]{2,0,1:T(8,128)(2,1)}, u32[]{:S(2)}, u32[]{:S(2)}) collective-permute-start(bf16[1024,16,256]{2,0,1:T(8,128)(2,1)} %copy.39), channel_id=1, source_target_pairs={{0,1},{1,2},{2,3},{3,0},{4,5},{5,6},{6,7},{7,4}} | collective-permute-start | bytes 25165832 | tf_op jit(solution)/shard_map/while/body/eval_jaxpr/while/body/eval_jaxpr/ppermute | solution.py:51
  600.4 183.6 %collective-permute-start.4 = (bf16[1024,16,256]{2,0,1:T(8,128)(2,1)}, bf16[1024,16,256]{2,0,1:T(8,128)(2,1)}, u32[]{:S(2)}, u32[]{:S(2)}) collective-permute-start(bf16[1024,16,256]{2,0,1:T(8,128)(2,1)} %get-tuple-element.109), channel_id=1, source_target_pairs={{0,4},{4,0},{1,5},{5,1},{2,6},{6,2},{3,7},{7,3}} | collective-permute-start | bytes 25165832 | tf_op jit(solution)/shard_map/while/body/eval_jaxpr/ppermute | solution.py:60
  602.8 359.7 %collective-permute-start.5 = (bf16[1024,16,256]{2,0,1:T(8,128)(2,1)}, bf16[1024,16,256]{2,0,1:T(8,128)(2,1)}, u32[]{:S(2)}, u32[]{:S(2)}) collective-permute-start(bf16[1024,16,256]{2,0,1:T(8,128)(2,1)} %get-tuple-element.112), channel_id=1, source_target_pairs={{0,4},{4,0},{1,5},{5,1},{2,6},{6,2},{3,7},{7,3}} | collective-permute-start | bytes 25165832 | tf_op jit(solution)/shard_map/while/body/eval_jaxpr/ppermute | solution.py:61
  969.8 97.5 %collective-permute-start = (bf16[1024,16,256]{2,0,1:T(8,128)(2,1)}, bf16[1024,16,256]{2,0,1:T(8,128)(2,1)}, u32[]{:S(2)}, u32[]{:S(2)}) collective-permute-start(bf16[1024,16,256]{2,0,1:T(8,128)(2,1)} %copy.56), channel_id=1, source_target_pairs={{0,1},{1,2},{2,3},{3,0},{4,5},{5,6},{6,7},{7,4}} | collective-permute-start | bytes 25165832 | tf_op jit(solution)/shard_map/while/body/eval_jaxpr/ppermute | solution.py:50
  977.2 175.3 %collective-permute-start.1 = (bf16[1024,16,256]{2,0,1:T(8,128)(2,1)}, bf16[1024,16,256]{2,0,1:T(8,128)(2,1)}, u32[]{:S(2)}, u32[]{:S(2)}) collective-permute-start(bf16[1024,16,256]{2,0,1:T(8,128)(2,1)} %copy.57), channel_id=1, source_target_pairs={{0,1},{1,2},{2,3},{3,0},{4,5},{5,6},{6,7},{7,4}} | collective-permute-start | bytes 25165832 | tf_op jit(solution)/shard_map/while/body/eval_jaxpr/ppermute | solution.py:51
  1159.9 97.5 %collective-permute-start = (bf16[1024,16,256]{2,0,1:T(8,128)(2,1)}, bf16[1024,16,256]{2,0,1:T(8,128)(2,1)}, u32[]{:S(2)}, u32[]{:S(2)}) collective-permute-start(bf16[1024,16,256]{2,0,1:T(8,128)(2,1)} %copy.56), channel_id=1, source_target_pairs={{0,1},{1,2},{2,3},{3,0},{4,5},{5,6},{6,7},{7,4}} | collective-permute-start | bytes 25165832 | tf_op jit(solution)/shard_map/while/body/eval_jaxpr/ppermute | solution.py:50
  1167.3 175.3 %collective-permute-start.1 = (bf16[1024,16,256]{2,0,1:T(8,128)(2,1)}, bf16[1024,16,256]{2,0,1:T(8,128)(2,1)}, u32[]{:S(2)}, u32[]{:S(2)}) collective-permute-start(bf16[1024,16,256]{2,0,1:T(8,128)(2,1)} %copy.57), channel_id=1, source_target_pairs={{0,1},{1,2},{2,3},{3,0},{4,5},{5,6},{6,7},{7,4}} | collective-permute-start | bytes 25165832 | tf_op jit(solution)/shard_map/while/body/eval_jaxpr/ppermute | solution.py:51
  1349.9 97.5 %collective-permute-start = (bf16[1024,16,256]{2,0,1:T(8,128)(2,1)}, bf16[1024,16,256]{2,0,1:T(8,128)(2,1)}, u32[]{:S(2)}, u32[]{:S(2)}) collective-permute-start(bf16[1024,16,256]{2,0,1:T(8,128)(2,1)} %copy.56), channel_id=1, source_target_pairs={{0,1},{1,2},{2,3},{3,0},{4,5},{5,6},{6,7},{7,4}} | collective-permute-start | bytes 25165832 | tf_op jit(solution)/shard_map/while/body/eval_jaxpr/ppermute | solution.py:50
  1357.3 175.3 %collective-permute-start.1 = (bf16[1024,16,256]{2,0,1:T(8,128)(2,1)}, bf16[1024,16,256]{2,0,1:T(8,128)(2,1)}, u32[]{:S(2)}, u32[]{:S(2)}) collective-permute-start(bf16[1024,16,256]{2,0,1:T(8,128)(2,1)} %copy.57), channel_id=1, source_target_pairs={{0,1},{1,2},{2,3},{3,0},{4,5},{5,6},{6,7},{7,4}} | collective-permute-start | bytes 25165832 | tf_op jit(solution)/shard_map/while/body/eval_jaxpr/ppermute | solution.py:51
where the time goes:
time: 1640 us; the launch traced here: 1630 us
  waiting for transfers between devices  786 us (48%)
  matrix products  523 us (32%)
  other arithmetic  180 us (11%)
  local copies, waits for them, and re-layouts  131 us (8%)
    ppermute x6, waiting for transfers between devices, step_x(): v_blk = lax.ppermute(v_blk, 'cx', perm_x)  516 us
    dot_general x8, matrix products, block_update(): jnp.einsum('kgqs,skd->kgqd', prob_blk.astype(jnp.bfloat16), v_blk, prefer...  294 us
    dot_general x8, matrix products, block_update(): jnp.einsum('qkgd,skd->kgqs', q_grouped, k_blk, preferred_element_type=jnp...  229 us
    ppermute x1, waiting for transfers between devices, step_y(): v_blk = lax.ppermute(v_blk, 'cy', perm_y)  178 us
    reduce_sum x8, other arithmetic, block_update(): row_sum = row_sum * rescale + jnp.sum(prob_blk, axis=-1)  171 us
    ppermute x1, waiting for transfers between devices, step_y(): k_blk = lax.ppermute(k_blk, 'cy', perm_y)  92 us
    while x12, local copies, waits for them, and re-layouts  46 us
    another operation x6, local copies, waits for them, and re-layouts  44.2 us
  transfers between devices with their start and end apart: 14, of which 8 were waited for; matrix products, arithmetic and copies ran while one was open for 41% of the time, Pallas kernels for 0%

commit v1 on v0

v1 whole, which is shorter than its diff:
```python
import functools
import math
import jax
import jax.numpy as jnp
from jax import lax
from jax.experimental import pallas as pl
from jax.experimental.pallas import tpu as pltpu
from jax.sharding import PartitionSpec as P

MESH = pl.DeviceIdType.MESH
KV_TILE = 512
UNROLL = 2
K_IDX, V_IDX, Q_IDX = 0, 1, 2
SEND_ORDER = (6, 2, 4, 7, 3, 5, 1)


def attend(scale, q, k_at, v_at, num_tiles, row_max, row_sum, out_acc, scores_buf):
    def scores_of(tile):
        return lax.dot_general(q, k_at(tile), (((1,), (1,)), ((), ())), preferred_element_type=jnp.float32)

    row_max[...] = jnp.full_like(row_max, -jnp.inf)
    row_sum[...] = jnp.zeros_like(row_sum)
    out_acc[...] = jnp.zeros_like(out_acc)
    scores_buf[0] = scores_of(0)

    def step(trip, carry):
        for part in range(UNROLL):
            tile = trip * UNROLL + part
            scores_buf[(part + 1) % 2] = scores_of(jnp.minimum(tile + 1, num_tiles - 1))
            scores = scores_buf[part % 2]
            old_max = row_max[...]
            new_max = jnp.maximum(old_max, jnp.max(scores, axis=1, keepdims=True) * scale)
            rescale = jnp.exp2(old_max - new_max)
            prob = jnp.exp2(scores * scale - jnp.tile(new_max, (1, KV_TILE // 128)))
            lanes = prob[:, :128]
            for c in range(1, KV_TILE // 128):
                lanes = lanes + prob[:, c * 128 : (c + 1) * 128]
            row_sum[...] = row_sum[...] * rescale + lanes
            row_max[...] = new_max
            weighted = lax.dot_general(
                prob.astype(jnp.bfloat16), v_at(tile), (((1,), (0,)), ((), ())), preferred_element_type=jnp.float32
            )
            out_acc[...] = out_acc[...] * jnp.tile(rescale, (1, out_acc.shape[1] // 128)) + weighted
        return carry

    lax.fori_loop(0, num_tiles // UNROLL, step, 0)
    total = jnp.sum(row_sum[...], axis=1, keepdims=True)
    return (out_acc[...] / total).astype(jnp.bfloat16)


def kernel(
    k_hbm, v_hbm, q_hbm, o_hbm, k_buf, v_buf, q_buf, o_buf, row_max, row_sum, out_acc, scores_buf, send_sem, recv_sem
):
    heads, tokens, head_dim = k_hbm.shape[1:]
    iy, ix = lax.axis_index("cy"), lax.axis_index("cx")
    me = ix * 2 + iy
    batch = lax.axis_index("batch")
    sources = (k_hbm, v_hbm, q_hbm)
    buffers = (k_buf, v_buf, q_buf)

    def peer(slot):
        px = (ix // 2 + slot // 4) % 2
        pc = (ix % 2 + slot % 2) % 2
        py = (iy + (slot // 2) % 2) % 2
        return px * 2 + pc, py

    def fetch(kind, head, slot):
        cx, cy = peer(slot)
        return pltpu.make_async_remote_copy(
            src_ref=sources[kind].at[cx * 2 + cy, head],
            dst_ref=buffers[kind].at[head, slot],
            send_sem=send_sem.at[kind, head, slot],
            recv_sem=recv_sem.at[kind, head, slot],
            device_id=(batch, cy, cx),
            device_id_type=MESH,
        )

    def fetch_own(kind, head):
        return pltpu.make_async_copy(
            sources[kind].at[me, head], buffers[kind].at[head, 0], recv_sem.at[kind, head, 0]
        )

    def give(head, slot):
        cx, cy = peer(slot)
        return pltpu.make_async_remote_copy(
            src_ref=o_buf.at[head, slot],
            dst_ref=o_hbm.at[me, head],
            send_sem=send_sem.at[3, head, slot],
            recv_sem=recv_sem.at[3, head, slot],
            device_id=(batch, cy, cx),
            device_id_type=MESH,
        )

    def give_own(head):
        return pltpu.make_async_copy(o_buf.at[head, 0], o_hbm.at[me, head], recv_sem.at[3, head, 0])

    barrier = pltpu.get_barrier_semaphore()
    for slot in range(1, 8):
        cx, cy = peer(slot)
        pl.semaphore_signal(barrier, inc=1, device_id=(batch, cy, cx), device_id_type=MESH)
    pl.semaphore_wait(barrier, 7)

    for head in range(heads):
        for kind in (K_IDX, V_IDX, Q_IDX):
            fetch_own(kind, head).start()
            for slot in SEND_ORDER:
                fetch(kind, head, slot).start()

    scale = math.log2(math.e) / math.sqrt(head_dim)
    per_slot = tokens // KV_TILE

    def rows(tile):
        return pl.ds(pl.multiple_of((tile % per_slot) * KV_TILE, KV_TILE), KV_TILE)

    def one_head(head, carry):
        for kind in (K_IDX, V_IDX):
            fetch_own(kind, head).wait()
            for slot in range(1, 8):
                fetch(kind, head, slot).wait_recv()

        def one_slot(turn, carry):
            slot = turn + head * (7 - 2 * turn)

            @pl.when(slot == 0)
            def _():
                fetch_own(Q_IDX, head).wait()

            @pl.when(slot != 0)
            def _():
                fetch(Q_IDX, head, slot).wait_recv()

            o_buf[head, slot] = attend(
                scale,
                q_buf[head, slot],
                lambda tile: k_buf[head, tile // per_slot, rows(tile), :],
                lambda tile: v_buf[head, tile // per_slot, rows(tile), :],
                8 * per_slot,
                row_max,
                row_sum,
                out_acc,
                scores_buf,
            )

            @pl.when(slot == 0)
            def _():
                give_own(head).start()

            @pl.when(slot != 0)
            def _():
                give(head, slot).start()

            return carry

        return lax.fori_loop(0, 8, one_slot, carry)

    lax.fori_loop(0, heads, one_head, 0)

    for head in range(heads):
        give_own(head).wait()
        for slot in range(1, 8):
            for kind in (K_IDX, V_IDX, Q_IDX):
                fetch(kind, head, slot).wait_send()
            give(head, slot).wait_send()
            give(head, slot).wait_recv()


def solution(mesh):
    group = mesh.shape["cx"] * mesh.shape["cy"]
    seq_spec = P(("batch", "cx", "cy"), None, None)

    def local_attention(q_local, k_local, v_local):
        tokens, num_heads, head_dim = q_local.shape
        heads = num_heads // group
        blocks = (heads, group, tokens, head_dim)

        def by_head(x):
            return jnp.transpose(x, (1, 0, 2)).reshape(group, heads, tokens, head_dim)

        out = pl.pallas_call(
            kernel,
            out_shape=jax.ShapeDtypeStruct((group, heads, tokens, head_dim), jnp.bfloat16),
            in_specs=[pl.BlockSpec(memory_space=pl.ANY)] * 3,
            out_specs=pl.BlockSpec(memory_space=pl.ANY),
            scratch_shapes=[
                pltpu.VMEM(blocks, jnp.bfloat16),
                pltpu.VMEM(blocks, jnp.bfloat16),
                pltpu.VMEM(blocks, jnp.bfloat16),
                pltpu.VMEM(blocks, jnp.bfloat16),
                pltpu.VMEM((tokens, 128), jnp.float32),
                pltpu.VMEM((tokens, 128), jnp.float32),
                pltpu.VMEM((tokens, head_dim), jnp.float32),
                pltpu.VMEM((2, tokens, KV_TILE), jnp.float32),
                pltpu.SemaphoreType.DMA((4, heads, group)),
                pltpu.SemaphoreType.DMA((4, heads, group)),
            ],
            compiler_params=pltpu.CompilerParams(
                collective_id=0, has_side_effects=True, vmem_limit_bytes=60 * 2**20
            ),
        )(by_head(k_local), by_head(v_local), by_head(q_local))
        return jnp.transpose(out.reshape(num_heads, tokens, head_dim), (1, 0, 2))

    return jax.shard_map(
        local_attention, mesh=mesh, in_specs=(seq_spec, seq_spec, seq_spec), out_specs=seq_spec, check_vma=False
    )
```

time: 1640 us -> 411 us (0.25)
  waiting for transfers between devices: 786 us -> 0 us
  matrix products: 523 us -> 0 us
  Pallas kernels: 0 us -> 370 us
  other arithmetic: 180 us -> 0 us
  local copies, waits for them, and re-layouts: 131 us -> 40.5 us
    ppermute x14 -> x0, waiting for transfers between devices: 786 us -> none  [the longest x6 516 us: step_x(): v_blk = lax.ppermute(v_blk, 'cx', perm_x)]
    dot_general x16 -> x0, matrix products: 523 us -> none  [the longest x8 294 us: block_update(): jnp.einsum('kgqs,skd->kgqd', prob_blk.astype(jnp.bfloat16), v_blk, prefer...]
    pallas_call x0 -> x1, Pallas kernels: none -> 370 us  [local_attention(): pl.pallas_call(kernel, out_shape=jax.ShapeDtypeStruct((group, heads, toke...]
    reduce_sum x8 -> x0, other arithmetic: 171 us -> none  [block_update(): row_sum = row_sum * rescale + jnp.sum(prob_blk, axis=-1)]
    while x12 -> x0, local copies, waits for them, and re-layouts: 46 us -> none
    another operation x6 -> x0, local copies, waits for them, and re-layouts: 44.2 us -> none
    unnamed x3 -> x0, local copies, waits for them, and re-layouts: 29.1 us -> none
    transpose x0 -> x3, local copies, waits for them, and re-layouts: none -> 29 us  [by_head(): return jnp.transpose(x, (1, 0, 2)).reshape(group, heads, tokens, head_dim)]
  transfers between devices with their start and end apart: 14 -> 0, of which waited for: 8 -> 0; matrix products, arithmetic and copies ran while one was open for 41% -> 0% of each run, Pallas kernels for 0% -> 0%
where the time goes in v1:
time: 411 us
  Pallas kernels  370 us (90%)
  local copies, waits for them, and re-layouts  40.5 us (10%)
    pallas_call x1, Pallas kernels, local_attention(): pl.pallas_call(kernel, out_shape=jax.ShapeDtypeStruct((group, heads, toke...  370 us
    transpose x3, local copies, waits for them, and re-layouts, by_head(): return jnp.transpose(x, (1, 0, 2)).reshape(group, heads, tokens, head_dim)  29 us
    reshape x1, local copies, waits for them, and re-layouts, local_attention(): return jnp.transpose(out.reshape(num_heads, tokens, head_dim), (1, 0, 2))  11.5 us

profile of v1, /device:TPU:0, one launch (start us, length us, event | category | flops | bytes accessed | tf_op | source)
XLA Modules:
  0.0 410.7 jit_solution(11858857964231401263)
XLA Ops:
  0.0 9.6 %copy.6 = bf16[16,1024,256]{2,1,0:T(8,128)(2,1)} copy(bf16[16,1024,256]{2,0,1:T(8,128)(2,1)} %bitcast.14) | data formatting | bytes 16777216 | tf_op jit(solution)/shard_map/transpose | solution.py:177
  9.6 9.8 %copy.4 = bf16[16,1024,256]{2,1,0:T(8,128)(2,1)} copy(bf16[16,1024,256]{2,0,1:T(8,128)(2,1)} %bitcast.15) | data formatting | bytes 16777216 | tf_op jit(solution)/shard_map/transpose | solution.py:177
  19.4 9.6 %copy.5 = bf16[16,1024,256]{2,1,0:T(8,128)(2,1)} copy(bf16[16,1024,256]{2,0,1:T(8,128)(2,1)} %bitcast.16) | data formatting | bytes 16777216 | tf_op jit(solution)/shard_map/transpose | solution.py:177
  29.0 370.1 %shard_map.37 = bf16[8,2,1024,256]{3,2,1,0:T(8,128)(2,1)} custom-call(bf16[8,2,1024,256]{3,2,1,0:T(8,128)(2,1)} %bitcast.12, bf16[8,2,1024,256]{3,2,1,0:T(8,128)(2,1)} %bitcast.13, bf16[8,2,1024,256]{3,2,1,0:T(8,128)(2,1)} %bitcast.11), custom_call_target="tpu_custom_call" | custom-call | tf_op jit(solution)/shard_map/pallas_call | solution.py:179
  399.1 11.5 %copy.9 = bf16[16,1024,256]{2,0,1:T(8,128)(2,1)} copy(bf16[16,1024,256]{2,1,0:T(8,128)(2,1)} %bitcast.10) | data formatting | bytes 16777216 | tf_op jit(solution)/shard_map/reshape | solution.py:200

commit v2 on v1

--- a/solution.py
+++ b/solution.py
@@ -10,6 +10,8 @@
 MESH = pl.DeviceIdType.MESH
 KV_TILE = 512
 UNROLL = 2
+TOKEN_TILE = 128
+TOKEN_GROUP = 16
 K_IDX, V_IDX, Q_IDX = 0, 1, 2
 SEND_ORDER = (6, 2, 4, 7, 3, 5, 1)
 
@@ -49,14 +51,16 @@
 
 
 def kernel(
-    k_hbm, v_hbm, q_hbm, o_hbm, k_buf, v_buf, q_buf, o_buf, row_max, row_sum, out_acc, scores_buf, send_sem, recv_sem
+    k_hbm, v_hbm, q_hbm, o_hbm,
+    k_buf, v_buf, q_buf, stage, landing, row_max, row_sum, out_acc, scores_buf, send_sem, recv_sem, load_sem,
 ):
-    heads, tokens, head_dim = k_hbm.shape[1:]
+    heads, group, tokens, head_dim = k_buf.shape
     iy, ix = lax.axis_index("cy"), lax.axis_index("cx")
     me = ix * 2 + iy
     batch = lax.axis_index("batch")
     sources = (k_hbm, v_hbm, q_hbm)
     buffers = (k_buf, v_buf, q_buf)
+    num_loads = tokens // TOKEN_TILE
 
     def peer(slot):
         px = (ix // 2 + slot // 4) % 2
@@ -64,11 +68,11 @@
         py = (iy + (slot // 2) % 2) % 2
         return px * 2 + pc, py
 
-    def fetch(kind, head, slot):
+    def fetch(kind, head, slot, span=slice(None)):
         cx, cy = peer(slot)
         return pltpu.make_async_remote_copy(
-            src_ref=sources[kind].at[cx * 2 + cy, head],
-            dst_ref=buffers[kind].at[head, slot],
+            src_ref=stage.at[kind, cx * 2 + cy, head, span],
+            dst_ref=buffers[kind].at[head, slot, span],
             send_sem=send_sem.at[kind, head, slot],
             recv_sem=recv_sem.at[kind, head, slot],
             device_id=(batch, cy, cx),
@@ -77,13 +81,18 @@
 
     def fetch_own(kind, head):
         return pltpu.make_async_copy(
-            sources[kind].at[me, head], buffers[kind].at[head, 0], recv_sem.at[kind, head, 0]
+            stage.at[kind, me, head], buffers[kind].at[head, 0], recv_sem.at[kind, head, 0]
         )
+
+    def fetch_all(kind, head):
+        fetch_own(kind, head).start()
+        for slot in SEND_ORDER:
+            fetch(kind, head, slot).start()
 
     def give(head, slot):
         cx, cy = peer(slot)
         return pltpu.make_async_remote_copy(
-            src_ref=o_buf.at[head, slot],
+            src_ref=stage.at[K_IDX, cx * 2 + cy, head],
             dst_ref=o_hbm.at[me, head],
             send_sem=send_sem.at[3, head, slot],
             recv_sem=recv_sem.at[3, head, slot],
@@ -92,19 +101,66 @@
         )
 
     def give_own(head):
-        return pltpu.make_async_copy(o_buf.at[head, 0], o_hbm.at[me, head], recv_sem.at[3, head, 0])
-
+        return pltpu.make_async_copy(stage.at[K_IDX, me, head], o_hbm.at[me, head], recv_sem.at[3, head, 0])
+
+    def token_span(tile):
+        return pl.ds(pl.multiple_of(tile * TOKEN_TILE, TOKEN_TILE), TOKEN_TILE)
+
+    def load(kind, tile):
+        return pltpu.make_async_copy(
+            sources[kind].at[token_span(tile)], landing.at[tile % 2], load_sem.at[tile % 2]
+        )
+
+    load(K_IDX, 0).start()
     barrier = pltpu.get_barrier_semaphore()
     for slot in range(1, 8):
         cx, cy = peer(slot)
         pl.semaphore_signal(barrier, inc=1, device_id=(batch, cy, cx), device_id_type=MESH)
     pl.semaphore_wait(barrier, 7)
 
-    for head in range(heads):
-        for kind in (K_IDX, V_IDX, Q_IDX):
-            fetch_own(kind, head).start()
-            for slot in SEND_ORDER:
-                fetch(kind, head, slot).start()
+    def send_first(tile):
+        for slot in SEND_ORDER:
+            fetch(K_IDX, 0, slot, token_span(tile)).start()
+
+    for kind in (K_IDX, V_IDX, Q_IDX):
+
+        def relayout(tile, carry):
+            @pl.when(tile + 1 < num_loads)
+            def _():
+                load(kind, tile + 1).start()
+
+            if kind != Q_IDX:
+
+                @pl.when(tile + 1 == num_loads)
+                def _():
+                    load(kind + 1, 0).start()
+
+            load(kind, tile).wait()
+
+            def some_tokens(part, carry):
+                rows = pl.ds(pl.multiple_of(part * TOKEN_GROUP, TOKEN_GROUP), TOKEN_GROUP)
+                first = pl.multiple_of(tile * TOKEN_TILE + part * TOKEN_GROUP, TOKEN_GROUP)
+                by_head = jnp.swapaxes(landing[tile % 2, rows], 0, 1)
+                stage[kind, :, :, pl.ds(first, TOKEN_GROUP), :] = by_head.reshape(group, heads, TOKEN_GROUP, head_dim)
+                return carry
+
+            lax.fori_loop(0, TOKEN_TILE // TOKEN_GROUP, some_tokens, 0)
+
+            if kind == K_IDX:
+
+                @pl.when(tile > 0)
+                def _():
+                    send_first(tile - 1)
+
+            return carry
+
+        lax.fori_loop(0, num_loads, relayout, 0)
+        if kind == V_IDX:
+            send_first(num_loads - 1)
+            fetch_own(K_IDX, 0).start()
+
+    for kind, head in ((V_IDX, 0), (Q_IDX, 0), (K_IDX, 1), (V_IDX, 1), (Q_IDX, 1)):
+        fetch_all(kind, head)
 
     scale = math.log2(math.e) / math.sqrt(head_dim)
     per_slot = tokens // KV_TILE
@@ -120,6 +176,7 @@
 
         def one_slot(turn, carry):
             slot = turn + head * (7 - 2 * turn)
+            cx, cy = peer(slot)
 
             @pl.when(slot == 0)
             def _():
@@ -128,8 +185,9 @@
             @pl.when(slot != 0)
             def _():
                 fetch(Q_IDX, head, slot).wait_recv()
-
-            o_buf[head, slot] = attend(
+                fetch(K_IDX, head, slot).wait_send()
+
+            stage[K_IDX, cx * 2 + cy, head] = attend(
                 scale,
                 q_buf[head, slot],
                 lambda tile: k_buf[head, tile // per_slot, rows(tile), :],
@@ -158,10 +216,42 @@
     for head in range(heads):
         give_own(head).wait()
         for slot in range(1, 8):
-            for kind in (K_IDX, V_IDX, Q_IDX):
+            for kind in (V_IDX, Q_IDX):
                 fetch(kind, head, slot).wait_send()
             give(head, slot).wait_send()
             give(head, slot).wait_recv()
+
+
+def by_token(o_hbm, out_hbm, o_buf, out_buf, in_sem, out_sem):
+    num_tiles = o_hbm.shape[1] // TOKEN_TILE
+
+    def span(tile):
+        return pl.ds(pl.multiple_of(tile * TOKEN_TILE, TOKEN_TILE), TOKEN_TILE)
+
+    def take(tile):
+        return pltpu.make_async_copy(o_hbm.at[:, span(tile)], o_buf.at[:, span(tile)], in_sem.at[tile])
+
+    def put(tile):
+        return pltpu.make_async_copy(out_buf.at[span(tile)], out_hbm.at[span(tile)], out_sem.at[tile])
+
+    for tile in range(num_tiles):
+        take(tile).start()
+
+    def one_tile(tile, carry):
+        take(tile).wait()
+
+        def some_tokens(part, carry):
+            rows = pl.ds(pl.multiple_of(tile * TOKEN_TILE + part * TOKEN_GROUP, TOKEN_GROUP), TOKEN_GROUP)
+            out_buf[rows] = jnp.swapaxes(o_buf[:, rows], 0, 1)
+            return carry
+
+        lax.fori_loop(0, TOKEN_TILE // TOKEN_GROUP, some_tokens, 0)
+        put(tile).start()
+        return carry
+
+    lax.fori_loop(0, num_tiles, one_tile, 0)
+    for tile in range(num_tiles):
+        put(tile).wait()
 
 
 def solution(mesh):
@@ -172,32 +262,44 @@
         tokens, num_heads, head_dim = q_local.shape
         heads = num_heads // group
         blocks = (heads, group, tokens, head_dim)
-
-        def by_head(x):
-            return jnp.transpose(x, (1, 0, 2)).reshape(group, heads, tokens, head_dim)
+        anywhere = pl.BlockSpec(memory_space=pl.ANY)
 
         out = pl.pallas_call(
             kernel,
             out_shape=jax.ShapeDtypeStruct((group, heads, tokens, head_dim), jnp.bfloat16),
-            in_specs=[pl.BlockSpec(memory_space=pl.ANY)] * 3,
-            out_specs=pl.BlockSpec(memory_space=pl.ANY),
+            in_specs=[anywhere] * 3,
+            out_specs=anywhere,
             scratch_shapes=[
                 pltpu.VMEM(blocks, jnp.bfloat16),
                 pltpu.VMEM(blocks, jnp.bfloat16),
                 pltpu.VMEM(blocks, jnp.bfloat16),
-                pltpu.VMEM(blocks, jnp.bfloat16),
+                pltpu.VMEM((3, group, heads, tokens, head_dim), jnp.bfloat16),
+                pltpu.VMEM((2, TOKEN_TILE, num_heads, head_dim), jnp.bfloat16),
                 pltpu.VMEM((tokens, 128), jnp.float32),
                 pltpu.VMEM((tokens, 128), jnp.float32),
                 pltpu.VMEM((tokens, head_dim), jnp.float32),
                 pltpu.VMEM((2, tokens, KV_TILE), jnp.float32),
                 pltpu.SemaphoreType.DMA((4, heads, group)),
                 pltpu.SemaphoreType.DMA((4, heads, group)),
+                pltpu.SemaphoreType.DMA((2,)),
             ],
             compiler_params=pltpu.CompilerParams(
-                collective_id=0, has_side_effects=True, vmem_limit_bytes=60 * 2**20
+                collective_id=0, has_side_effects=True, vmem_limit_bytes=67043328
             ),
-        )(by_head(k_local), by_head(v_local), by_head(q_local))
-        return jnp.transpose(out.reshape(num_heads, tokens, head_dim), (1, 0, 2))
+        )(k_local, v_local, q_local)
+        return pl.pallas_call(
+            by_token,
+            out_shape=jax.ShapeDtypeStruct(q_local.shape, jnp.bfloat16),
+            in_specs=[anywhere],
+            out_specs=anywhere,
+            scratch_shapes=[
+                pltpu.VMEM((num_heads, tokens, head_dim), jnp.bfloat16),
+                pltpu.VMEM((tokens, num_heads, head_dim), jnp.bfloat16),
+                pltpu.SemaphoreType.DMA((tokens // TOKEN_TILE,)),
+                pltpu.SemaphoreType.DMA((tokens // TOKEN_TILE,)),
+            ],
+            compiler_params=pltpu.CompilerParams(vmem_limit_bytes=48 * 2**20),
+        )(out.reshape(num_heads, tokens, head_dim))
 
     return jax.shard_map(
         local_attention, mesh=mesh, in_specs=(seq_spec, seq_spec, seq_spec), out_specs=seq_spec, check_vma=False

time: 411 us -> 380 us (0.925)
  local copies, waits for them, and re-layouts: 40.5 us -> 0 us
  Pallas kernels: 370 us -> 379 us
    transpose x3 -> x0, local copies, waits for them, and re-layouts: 29 us -> none  [by_head(): return jnp.transpose(x, (1, 0, 2)).reshape(group, heads, tokens, head_dim)]
    reshape x1 -> x0, local copies, waits for them, and re-layouts: 11.5 us -> none  [local_attention(): return jnp.transpose(out.reshape(num_heads, tokens, head_dim), (1, 0, 2))]
    pallas_call x0 -> x1, Pallas kernels: none -> 7.03 us  [local_attention(): pl.pallas_call(by_token, out_shape=jax.ShapeDtypeStruct(q_local.shape, jn...]
where the time goes in v2:
time: 380 us; the launch traced here: 379 us
  Pallas kernels  379 us (100%)
    pallas_call x1, Pallas kernels, local_attention(): pl.pallas_call(kernel, out_shape=jax.ShapeDtypeStruct((group, heads, toke...  372 us

profile of v2, /device:TPU:0, one launch (start us, length us, event | category | flops | bytes accessed | tf_op | source)
XLA Modules:
  0.0 378.7 jit_solution(14865612612116155476)
XLA Ops:
  0.0 371.7 %shard_map.37 = bf16[8,2,1024,256]{3,2,1,0:T(8,128)(2,1)} custom-call(bf16[1024,16,256]{2,1,0:T(8,128)(2,1)} %k_hbm.1, bf16[1024,16,256]{2,1,0:T(8,128)(2,1)} %v_hbm.1, bf16[1024,16,256]{2,1,0:T(8,128)(2,1)} %q_hbm.1), custom_call_target="tpu_custom_call" | custom-call | tf_op jit(solution)/shard_map/pallas_call | solution.py:267
  371.7 7.0 %shard_map.38 = bf16[1024,16,256]{2,1,0:T(8,128)(2,1)} custom-call(bf16[16,1024,256]{2,1,0:T(8,128)(2,1)} %bitcast.1), custom_call_target="tpu_custom_call" | custom-call | tf_op jit(solution)/shard_map/pallas_call | solution.py:290

commit v3 on v2

v3 whole, which is shorter than its diff:
```python
import functools
import math
import jax
import jax.numpy as jnp
from jax import lax
from jax.experimental import pallas as pl
from jax.experimental.pallas import tpu as pltpu
from jax.sharding import PartitionSpec as P

MESH = pl.DeviceIdType.MESH
KV_TILE = 512
UNROLL = 4
TOKEN_TILE = 128
LOAD_TILE = 64
TOKEN_GROUP = 16
K_IDX, V_IDX, Q_IDX = 0, 1, 2
SEND_ORDER = (6, 2, 4, 7, 3, 5, 1)


def attend(scale, q_at, k_at, v_at, num_tiles, row_max, row_sum, out_acc, scores_buf):
    def scores_of(tile):
        return lax.dot_general(q_at(), k_at(tile), (((1,), (1,)), ((), ())), preferred_element_type=jnp.float32)

    row_max[...] = jnp.full_like(row_max, -jnp.inf)
    row_sum[...] = jnp.zeros_like(row_sum)
    out_acc[...] = jnp.zeros_like(out_acc)
    scores_buf[0] = scores_of(0)

    def step(trip, carry):
        for part in range(UNROLL):
            tile = trip * UNROLL + part
            scores_buf[(part + 1) % 2] = scores_of(jnp.minimum(tile + 1, num_tiles - 1))
            scores = scores_buf[part % 2]
            old_max = row_max[...]
            new_max = jnp.maximum(old_max, jnp.max(scores, axis=1, keepdims=True) * scale)
            rescale = jnp.exp2(old_max - new_max)
            prob = jnp.exp2(scores * scale - jnp.tile(new_max, (1, KV_TILE // 128)))
            lanes = prob[:, :128]
            for c in range(1, KV_TILE // 128):
                lanes = lanes + prob[:, c * 128 : (c + 1) * 128]
            row_sum[...] = row_sum[...] * rescale + lanes
            row_max[...] = new_max
            weighted = lax.dot_general(
                prob.astype(jnp.bfloat16), v_at(tile), (((1,), (0,)), ((), ())), preferred_element_type=jnp.float32
            )
            out_acc[...] = out_acc[...] * jnp.tile(rescale, (1, out_acc.shape[1] // 128)) + weighted
        return carry

    lax.fori_loop(0, num_tiles // UNROLL, step, 0)
    total = jnp.sum(row_sum[...], axis=1, keepdims=True)
    return (out_acc[...] / total).astype(jnp.bfloat16)


def kernel(
    k_hbm, v_hbm, q_hbm, o_home, pool, landing, row_max, row_sum, out_acc, scores_buf, send_sem, recv_sem, load_sem
):
    group, heads, tokens, head_dim = o_home.shape
    iy, ix = lax.axis_index("cy"), lax.axis_index("cx")
    me = ix * 2 + iy
    batch = lax.axis_index("batch")
    sources = (k_hbm, v_hbm, q_hbm)
    num_loads = tokens // LOAD_TILE

    def peer(slot):
        px = (ix // 2 + slot // 4) % 2
        pc = (ix % 2 + slot % 2) % 2
        py = (iy + (slot // 2) % 2) % 2
        return px * 2 + pc, py

    def block_of(slot):
        return (slot + group - 1) % (2 * group - 1) + (group - slot) // group * (me - group + 1)

    def fetch(kind, head, slot, span=slice(None)):
        cx, cy = peer(slot)
        return pltpu.make_async_remote_copy(
            src_ref=pool.at[kind, cx * 2 + cy, head, span],
            dst_ref=pool.at[kind, group - 1 + slot, head, span],
            send_sem=send_sem.at[kind, head, slot],
            recv_sem=recv_sem.at[kind, head, slot],
            device_id=(batch, cy, cx),
            device_id_type=MESH,
        )

    def fetch_all(kind, head):
        for slot in SEND_ORDER:
            fetch(kind, head, slot).start()

    def give(head, slot):
        cx, cy = peer(slot)
        return pltpu.make_async_remote_copy(
            src_ref=pool.at[Q_IDX, block_of(slot), head],
            dst_ref=o_home.at[me, head],
            send_sem=send_sem.at[3, head, slot],
            recv_sem=recv_sem.at[3, head, slot],
            device_id=(batch, cy, cx),
            device_id_type=MESH,
        )

    def give_own(head):
        return pltpu.make_async_copy(pool.at[Q_IDX, me, head], o_home.at[me, head], recv_sem.at[3, head, 0])

    def token_span(tile):
        return pl.ds(pl.multiple_of(tile * LOAD_TILE, LOAD_TILE), LOAD_TILE)

    def load(kind, tile):
        return pltpu.make_async_copy(
            sources[kind].at[token_span(tile)], landing.at[tile % 2], load_sem.at[tile % 2]
        )

    load(K_IDX, 0).start()
    barrier = pltpu.get_barrier_semaphore()
    for slot in range(1, 8):
        cx, cy = peer(slot)
        pl.semaphore_signal(barrier, inc=1, device_id=(batch, cy, cx), device_id_type=MESH)

    def send_first(tile):
        for slot in SEND_ORDER:
            fetch(K_IDX, 0, slot, token_span(tile)).start()

    for kind in (K_IDX, V_IDX, Q_IDX):

        def relayout(tile, carry):
            @pl.when(tile + 1 < num_loads)
            def _():
                load(kind, tile + 1).start()

            if kind != Q_IDX:

                @pl.when(tile + 1 == num_loads)
                def _():
                    load(kind + 1, 0).start()

            load(kind, tile).wait()

            def some_tokens(part, carry):
                rows = pl.ds(pl.multiple_of(part * TOKEN_GROUP, TOKEN_GROUP), TOKEN_GROUP)
                first = pl.multiple_of(tile * LOAD_TILE + part * TOKEN_GROUP, TOKEN_GROUP)
                by_head = jnp.swapaxes(landing[tile % 2, rows], 0, 1)
                pool[kind, :group, :, pl.ds(first, TOKEN_GROUP), :] = by_head.reshape(
                    group, heads, TOKEN_GROUP, head_dim
                )
                return carry

            lax.fori_loop(0, LOAD_TILE // TOKEN_GROUP, some_tokens, 0)

            if kind == K_IDX:

                @pl.when(tile == 0)
                def _():
                    pl.semaphore_wait(barrier, 7)

                @pl.when(tile > 0)
                def _():
                    send_first(tile - 1)

            return carry

        lax.fori_loop(0, num_loads, relayout, 0)
        if kind == V_IDX:
            send_first(num_loads - 1)

    for kind, head in ((V_IDX, 0), (Q_IDX, 0), (K_IDX, 1), (V_IDX, 1), (Q_IDX, 1)):
        fetch_all(kind, head)

    scale = math.log2(math.e) / math.sqrt(head_dim)
    per_slot = tokens // KV_TILE

    def rows(tile):
        return pl.ds(pl.multiple_of((tile % per_slot) * KV_TILE, KV_TILE), KV_TILE)

    def one_head(head, carry):
        for kind in (K_IDX, V_IDX):
            for slot in range(1, 8):
                fetch(kind, head, slot).wait_recv()

        @pl.when(head > 0)
        def _():
            give_own(head - 1).start()
            for slot in SEND_ORDER:
                give(head - 1, slot).start()

        def one_slot(turn, carry):
            slot = turn + head * (7 - 2 * turn)
            block = block_of(slot)

            @pl.when(slot != 0)
            def _():
                fetch(Q_IDX, head, slot).wait_recv()

            pool[Q_IDX, block, head] = attend(
                scale,
                lambda: pool[Q_IDX, block, head],
                lambda tile: pool[K_IDX, block_of(tile // per_slot), head, rows(tile), :],
                lambda tile: pool[V_IDX, block_of(tile // per_slot), head, rows(tile), :],
                group * per_slot,
                row_max,
                row_sum,
                out_acc,
                scores_buf,
            )

            @pl.when((head == heads - 1) & (slot == 0))
            def _():
                give_own(head).start()

            @pl.when((head == heads - 1) & (slot != 0))
            def _():
                give(head, slot).start()

            return carry

        return lax.fori_loop(0, 8, one_slot, carry)

    lax.fori_loop(0, heads, one_head, 0)

    for head in range(heads):
        give_own(head).wait()
        for slot in range(1, 8):
            for kind in (K_IDX, V_IDX, Q_IDX):
                fetch(kind, head, slot).wait_send()
            give(head, slot).wait_send()
            give(head, slot).wait_recv()


def by_token(o_buf, out_hbm, out_buf, out_sem):
    num_tiles = o_buf.shape[1] // TOKEN_TILE

    def put(tile):
        span = pl.ds(pl.multiple_of(tile * TOKEN_TILE, TOKEN_TILE), TOKEN_TILE)
        return pltpu.make_async_copy(out_buf.at[span], out_hbm.at[span], out_sem.at[tile])

    def one_tile(tile, carry):
        def some_tokens(part, carry):
            rows = pl.ds(pl.multiple_of(tile * TOKEN_TILE + part * TOKEN_GROUP, TOKEN_GROUP), TOKEN_GROUP)
            out_buf[rows] = jnp.swapaxes(o_buf[:, rows], 0, 1)
            return carry

        lax.fori_loop(0, TOKEN_TILE // TOKEN_GROUP, some_tokens, 0)
        put(tile).start()
        return carry

    lax.fori_loop(0, num_tiles, one_tile, 0)
    for tile in range(num_tiles):
        put(tile).wait()


def solution(mesh):
    group = mesh.shape["cx"] * mesh.shape["cy"]
    seq_spec = P(("batch", "cx", "cy"), None, None)

    def local_attention(q_local, k_local, v_local):
        tokens, num_heads, head_dim = q_local.shape
        heads = num_heads // group
        blocks = (group, heads, tokens, head_dim)
        anywhere = pl.BlockSpec(memory_space=pl.ANY)

        out = pl.pallas_call(
            kernel,
            out_shape=pltpu.VMEM(blocks, jnp.bfloat16),
            in_specs=[anywhere] * 3,
            out_specs=anywhere,
            scratch_shapes=[
                pltpu.VMEM((3, 2 * group - 1, heads, tokens, head_dim), jnp.bfloat16),
                pltpu.VMEM((2, LOAD_TILE, num_heads, head_dim), jnp.bfloat16),
                pltpu.VMEM((tokens, 128), jnp.float32),
                pltpu.VMEM((tokens, 128), jnp.float32),
                pltpu.VMEM((tokens, head_dim), jnp.float32),
                pltpu.VMEM((2, tokens, KV_TILE), jnp.float32),
                pltpu.SemaphoreType.DMA((4, heads, group)),
                pltpu.SemaphoreType.DMA((4, heads, group)),
                pltpu.SemaphoreType.DMA((2,)),
            ],
            compiler_params=pltpu.CompilerParams(
                collective_id=0, has_side_effects=True, vmem_limit_bytes=58600000
            ),
        )(k_local, v_local, q_local)
        return pl.pallas_call(
            by_token,
            out_shape=jax.ShapeDtypeStruct(q_local.shape, jnp.bfloat16),
            in_specs=[pl.BlockSpec(memory_space=pltpu.VMEM)],
            out_specs=anywhere,
            scratch_shapes=[
                pltpu.VMEM((tokens, num_heads, head_dim), jnp.bfloat16),
                pltpu.SemaphoreType.DMA((tokens // TOKEN_TILE,)),
            ],
            compiler_params=pltpu.CompilerParams(vmem_limit_bytes=24 * 2**20),
        )(out.reshape(num_heads, tokens, head_dim))

    return jax.shard_map(
        local_attention, mesh=mesh, in_specs=(seq_spec, seq_spec, seq_spec), out_specs=seq_spec, check_vma=False
    )
```

time: 380 us -> 372 us (0.979)
  Pallas kernels: 379 us -> 371 us
    pallas_call x1, Pallas kernels: 372 us -> 367 us  [local_attention(): pl.pallas_call(kernel, out_shape=pltpu.VMEM(blocks, jnp.bfloat16), in_spe...]
where the time goes in v3:
time: 372 us; the launch traced here: 371 us
  Pallas kernels  371 us (100%)
    pallas_call x1, Pallas kernels, local_attention(): pl.pallas_call(kernel, out_shape=pltpu.VMEM(blocks, jnp.bfloat16), in_spe...  367 us

profile of v3, /device:TPU:0, one launch (start us, length us, event | category | flops | bytes accessed | tf_op | source)
XLA Modules:
  0.0 371.2 jit_solution(11952235797066576657)
XLA Ops:
  0.0 367.5 %shard_map.37 = bf16[8,2,1024,256]{3,2,1,0:T(8,128)(2,1)S(1)} custom-call(bf16[1024,16,256]{2,1,0:T(8,128)(2,1)} %k_hbm.1, bf16[1024,16,256]{2,1,0:T(8,128)(2,1)} %v_hbm.1, bf16[1024,16,256]{2,1,0:T(8,128)(2,1)} %q_hbm.1), custom_call_target="tpu_custom_call" | custom-call | tf_op jit(solution)/shard_map/pallas_call | solution.py:257
  367.5 3.7 shard_map.38

commit v4 on v3

--- a/solution.py
+++ b/solution.py
@@ -10,7 +10,7 @@
 MESH = pl.DeviceIdType.MESH
 KV_TILE = 512
 UNROLL = 4
-TOKEN_TILE = 128
+TOKEN_TILE = 64
 LOAD_TILE = 64
 TOKEN_GROUP = 16
 K_IDX, V_IDX, Q_IDX = 0, 1, 2
@@ -21,7 +21,7 @@
     def scores_of(tile):
         return lax.dot_general(q_at(), k_at(tile), (((1,), (1,)), ((), ())), preferred_element_type=jnp.float32)
 
-    row_max[...] = jnp.full_like(row_max, -jnp.inf)
+    row_max[...] = jnp.full_like(row_max, jnp.finfo(jnp.float32).min)
     row_sum[...] = jnp.zeros_like(row_sum)
     out_acc[...] = jnp.zeros_like(out_acc)
     scores_buf[0] = scores_of(0)
@@ -32,9 +32,9 @@
             scores_buf[(part + 1) % 2] = scores_of(jnp.minimum(tile + 1, num_tiles - 1))
             scores = scores_buf[part % 2]
             old_max = row_max[...]
-            new_max = jnp.maximum(old_max, jnp.max(scores, axis=1, keepdims=True) * scale)
-            rescale = jnp.exp2(old_max - new_max)
-            prob = jnp.exp2(scores * scale - jnp.tile(new_max, (1, KV_TILE // 128)))
+            new_max = jnp.maximum(old_max, jnp.max(scores, axis=1, keepdims=True))
+            rescale = jnp.exp2((old_max - new_max) * scale)
+            prob = jnp.exp2((scores - jnp.tile(new_max, (1, KV_TILE // 128))) * scale)
             lanes = prob[:, :128]
             for c in range(1, KV_TILE // 128):
                 lanes = lanes + prob[:, c * 128 : (c + 1) * 128]
@@ -113,9 +113,11 @@
         cx, cy = peer(slot)
         pl.semaphore_signal(barrier, inc=1, device_id=(batch, cy, cx), device_id_type=MESH)
 
-    def send_first(tile):
+    def send_first(tile, count):
         for slot in SEND_ORDER:
-            fetch(K_IDX, 0, slot, token_span(tile)).start()
+            fetch(K_IDX, 0, slot, pl.ds(tile * LOAD_TILE, count * LOAD_TILE)).start()
+
+    first_spans = [(0, 1)] + [(1 << n, 1 << n) for n in range(num_loads.bit_length() - 1)]
 
     for kind in (K_IDX, V_IDX, Q_IDX):
 
@@ -145,19 +147,25 @@
 
             if kind == K_IDX:
 
+                @pl.when(tile == 1)
+                def _():
+                    pl.semaphore_wait(barrier, 7)
+
+                for begin, count in first_spans[:-1]:
+
+                    @pl.when(tile == begin + count)
+                    def _():
+                        send_first(begin, count)
+
+            if kind == V_IDX:
+
                 @pl.when(tile == 0)
                 def _():
-                    pl.semaphore_wait(barrier, 7)
-
-                @pl.when(tile > 0)
-                def _():
-                    send_first(tile - 1)
+                    send_first(*first_spans[-1])
 
             return carry
 
         lax.fori_loop(0, num_loads, relayout, 0)
-        if kind == V_IDX:
-            send_first(num_loads - 1)
 
     for kind, head in ((V_IDX, 0), (Q_IDX, 0), (K_IDX, 1), (V_IDX, 1), (Q_IDX, 1)):
         fetch_all(kind, head)
@@ -203,9 +211,9 @@
             def _():
                 give_own(head).start()
 
-            @pl.when((head == heads - 1) & (slot != 0))
-            def _():
-                give(head, slot).start()
+            @pl.when((head == heads - 1) & (turn > 0))
+            def _():
+                give(head, slot + 1).start()
 
             return carry
 
@@ -235,7 +243,7 @@
             out_buf[rows] = jnp.swapaxes(o_buf[:, rows], 0, 1)
             return carry
 
-        lax.fori_loop(0, TOKEN_TILE // TOKEN_GROUP, some_tokens, 0)
+        lax.fori_loop(0, TOKEN_TILE // TOKEN_GROUP, some_tokens, 0, unroll=2)
         put(tile).start()
         return carry
 

time: 372 us -> 372 us (level)
  no operation moved by 1% of the time
where the time goes in v4:
time: 372 us; the launch traced here: 371 us
  Pallas kernels  371 us (100%)
    pallas_call x1, Pallas kernels, local_attention(): pl.pallas_call(kernel, out_shape=pltpu.VMEM(blocks, jnp.bfloat16), in_spe...  368 us

profile of v4, /device:TPU:0, one launch (start us, length us, event | category | flops | bytes accessed | tf_op | source)
XLA Modules:
  0.0 371.2 jit_solution(16519098062692034472)
XLA Ops:
  0.0 367.6 %shard_map.37 = bf16[8,2,1024,256]{3,2,1,0:T(8,128)(2,1)S(1)} custom-call(bf16[1024,16,256]{2,1,0:T(8,128)(2,1)} %k_hbm.1, bf16[1024,16,256]{2,1,0:T(8,128)(2,1)} %v_hbm.1, bf16[1024,16,256]{2,1,0:T(8,128)(2,1)} %q_hbm.1), custom_call_target="tpu_custom_call" | custom-call | tf_op jit(solution)/shard_map/pallas_call | solution.py:265
  367.6 3.6 shard_map.38

commit v5 on v4

--- a/solution.py
+++ b/solution.py
@@ -143,7 +143,7 @@
                 )
                 return carry
 
-            lax.fori_loop(0, LOAD_TILE // TOKEN_GROUP, some_tokens, 0)
+            lax.fori_loop(0, LOAD_TILE // TOKEN_GROUP, some_tokens, 0, unroll=LOAD_TILE // TOKEN_GROUP)
 
             if kind == K_IDX:
 
@@ -243,7 +243,7 @@
             out_buf[rows] = jnp.swapaxes(o_buf[:, rows], 0, 1)
             return carry
 
-        lax.fori_loop(0, TOKEN_TILE // TOKEN_GROUP, some_tokens, 0, unroll=2)
+        lax.fori_loop(0, TOKEN_TILE // TOKEN_GROUP, some_tokens, 0, unroll=TOKEN_TILE // TOKEN_GROUP)
         put(tile).start()
         return carry
 

time: 372 us -> 372 us (level)
  no operation moved by 1% of the time
where the time goes in v5:
time: 372 us; the launch traced here: 371 us
  Pallas kernels  371 us (100%)
    pallas_call x1, Pallas kernels, local_attention(): pl.pallas_call(kernel, out_shape=pltpu.VMEM(blocks, jnp.bfloat16), in_spe...  368 us

profile of v5, /device:TPU:0, one launch (start us, length us, event | category | flops | bytes accessed | tf_op | source)
XLA Modules:
  0.0 371.1 jit_solution(12436505457569193256)
XLA Ops:
  0.0 367.5 %shard_map.37 = bf16[8,2,1024,256]{3,2,1,0:T(8,128)(2,1)S(1)} custom-call(bf16[1024,16,256]{2,1,0:T(8,128)(2,1)} %k_hbm.1, bf16[1024,16,256]{2,1,0:T(8,128)(2,1)} %v_hbm.1, bf16[1024,16,256]{2,1,0:T(8,128)(2,1)} %q_hbm.1), custom_call_target="tpu_custom_call" | custom-call | tf_op jit(solution)/shard_map/pallas_call | solution.py:265
  367.6 3.5 shard_map.38
